TPU v7x, 32 devices: a whole 2x2x4 slice. The times are simulated.
32 devices in a mesh: dp: 8 (over z, y), tensor: 4 (over x, core).
Axes of the slice: x: 2, y: 2, z: 4, core: 2. Of those that a mesh axis runs over, the one named last changes fastest.
Arguments:
- patches: bfloat16 [8192, 1280], P('dp'), may hold values from -27 to 27
- norm_gain: float32 [1280], replicated, may hold values from 0.1 to 1.9
- norm_bias: float32 [1280], replicated, may hold values from -3 to 3
- first_weight: bfloat16 [5120, 5120], P(None, 'tensor'), may hold values from -0.078125 to 0.078125
- first_bias: float32 [5120], P('tensor'), may hold values from -3 to 3
- second_weight: bfloat16 [5120, 8192], P('tensor', 'dp'), may hold values from -0.078125 to 0.078125
- second_bias: float32 [8192], P('tensor'), may hold values from -2 to 2
- text_embeds: bfloat16 [4096, 8192], P('dp', 'tensor'), may hold values from -36 to 36
- final_gain: float32 [8192], P('tensor'), may hold values from 0.1 to 1.9
- image_grids: int32 [8, 4, 2], replicated, may hold values from 2 to 8, as said below
- routing: int32 [8, 4], replicated, may hold values from 0 to 3, each once within a row
Outputs:
- embeddings: bfloat16 [4096, 8192], P('dp', 'tensor')
- normed: bfloat16 [4096, 8192], P('dp', 'tensor')
Inputs may be any that keep to these rules, and one draw needn't show every extreme that they name: `image_grids`: each image is a grid of 3 to 8 rows by 2 to 8 columns of merged tokens; in every draw some image is 8 by 8. `routing`: each row names every offset 0 to 3 once.
All inputs are finite; a program needn't handle non-finite values.
Results may differ from a plain program's by a relative error of at most 0.006.
Values may be sent and summed in bfloat16 or wider, within the bound.
A program may use at most 128 MiB of HBM per device.

v0:
```python
import jax
import jax.numpy as jnp
from jax import lax
from jax.sharding import PartitionSpec as P

D = 8192


def passed_along(block, axis, distance):
    devices = range(lax.axis_size(axis))
    route = [((i - distance) % len(devices), i) for i in devices]
    return lax.ppermute(block, axis, route)


def per_device(
    patches,
    norm_gain,
    norm_bias,
    first_weight,
    first_bias,
    second_weight,
    second_bias,
    text_embeds,
    final_gain,
    image_grids,
    routing,
):
    patch_values = patches.astype(jnp.float32)
    centered = patch_values - jnp.mean(patch_values, axis=-1, keepdims=True)
    variance = jnp.mean(centered * centered, axis=-1, keepdims=True)
    normed_patches = centered * lax.rsqrt(variance + 1e-06) * norm_gain + norm_bias
    merged = normed_patches.reshape(-1, first_weight.shape[0]).astype(jnp.bfloat16)
    hidden = jax.nn.gelu(
        jnp.dot(merged, first_weight, preferred_element_type=jnp.float32) + first_bias,
        approximate=False,
    ).astype(jnp.bfloat16)
    own_index = lax.axis_index("dp")
    shard_count = lax.axis_size("dp")
    partial_value = jnp.dot(
        lax.all_gather(hidden, "dp", axis=0, tiled=True),
        second_weight,
        preferred_element_type=jnp.float32,
    ).astype(jnp.bfloat16)
    columns = lax.all_to_all(partial_value, "dp", split_axis=0, concat_axis=1, tiled=True)
    partial_terms = columns.astype(jnp.float32)
    summed = lax.psum_scatter(
        partial_terms.astype(jnp.bfloat16), "tensor", scatter_dimension=1, tiled=True
    ).astype(jnp.float32)
    projected = (summed + second_bias).astype(jnp.bfloat16)
    block_total = image_grids.shape[1]
    cap_rows = projected.shape[0] // block_total
    feature_width = projected.shape[1]
    block_rows = projected.reshape(block_total, cap_rows, feature_width)
    counts_all = image_grids[:, :, 0] * image_grids[:, :, 1]
    slot_ids = jnp.arange(block_total, dtype=jnp.int32)
    own_routing = lax.dynamic_index_in_dim(routing, own_index, 0, keepdims=False)
    seq_rows = text_embeds.shape[0]
    image_rows = jnp.zeros((seq_rows, feature_width), jnp.bfloat16)
    filled_rows = jnp.zeros((), jnp.int32)
    zero_index = jnp.zeros((), jnp.int32)
    for stride in range(block_total):
        own_block = jnp.sum(jnp.where(own_routing == stride, slot_ids, 0))
        outgoing = lax.dynamic_index_in_dim(block_rows, own_block, 0, keepdims=False)
        if stride > 0:
            incoming = passed_along(outgoing, "dp", stride)
        else:
            incoming = outgoing
        source_shard = (own_index - stride) % shard_count
        source_routing = lax.dynamic_index_in_dim(routing, source_shard, 0, keepdims=False)
        source_block = jnp.sum(jnp.where(source_routing == stride, slot_ids, 0))
        source_counts = lax.dynamic_index_in_dim(counts_all, source_shard, 0, keepdims=False)
        image_count = lax.dynamic_index_in_dim(source_counts, source_block, 0, keepdims=False)
        image_rows = lax.dynamic_update_slice(image_rows, incoming, (filled_rows, zero_index))
        filled_rows = filled_rows + image_count
    position = jnp.arange(seq_rows, dtype=jnp.int32)[:, None]
    embeddings = jnp.where(position < filled_rows, image_rows, text_embeds)
    embed_values = embeddings.astype(jnp.float32)
    square_total = lax.psum(jnp.sum(embed_values * embed_values, axis=-1), "tensor")
    scale_rows = lax.rsqrt(square_total / D + 1e-06)
    normed = (embed_values * scale_rows[:, None] * final_gain).astype(jnp.bfloat16)
    return (embeddings, normed)


def solution(mesh):
    placed = (
        P("dp", None),
        P(),
        P(),
        P(None, "tensor"),
        P("tensor"),
        P("tensor", "dp"),
        P("tensor"),
        P("dp", "tensor"),
        P("tensor"),
        P(),
        P(),
    )
    return jax.shard_map(
        per_device,
        mesh=mesh,
        in_specs=placed,
        out_specs=(P("dp", "tensor"), P("dp", "tensor")),
        check_vma=False,
    )
```

profile of v0, /device:TPU:0, one launch (start us, length us, event | category | flops | bytes accessed | tf_op | source)
XLA Modules:
  0.0 334.0 jit_solution(4629358095571909499)
XLA Ops:
  7.2 0.0 copy-start
  7.2 0.0 all-gather.2.cloned.1.call-start
  7.2 0.0 copy-start.1
  7.2 2.3 convert_reduce_fusion
  9.6 0.3 copy-done.1
  9.9 0.0 copy-start.3
  9.9 0.0 copy-start.4
  9.9 0.8 fusion.2
  10.7 0.0 copy-done.3
  10.8 0.0 copy-done.4
  10.8 2.5 fusion.5
  13.3 0.0 copy-start.8
  13.3 5.2 %convert_element_type.31 = bf16[256,5120]{1,0:T(8,128)(2,1)} reshape(bf16[1024,1280]{1,0:T(8,128)(2,1)} %fusion.5) | data formatting | bytes 5242880 | tf_op jit(solution)/shard_map/convert_element_type | solution.py:32
  18.5 0.0 copy-done.8
  18.5 12.5 %fusion.11 = bf16[256,1280]{1,0:T(8,128)(2,1)} fusion(bf16[256,5120]{1,0:T(8,128)(2,1)} %convert_element_type.31, bf16[5120,1280]{1,0:T(8,128)(2,1)} %param.14, f32[1280]{0:T(1024)S(1)} %copy-done.8), kind=kOutput, calls=%fused_computation.20 | convolution fusion | flops 3377070080 | bytes 16389120 | tf_op jit(solution)/shard_map/dot_general | solution.py:34
  31.1 0.0 all-gather.2.cloned.1.call-update
  31.1 0.0 reduce-scatter.2.cloned.1.call-start
  31.1 88.7 %all-gather.2.cloned.1.call-done = bf16[2048,1280]{1,0:T(8,128)(2,1)} async-done(((bf16[256,1280]{1,0:T(8,128)(2,1)}), bf16[2048,1280]{1,0:T(8,128)(2,1)}) %all-gather.2.cloned.1.call-update) | async-done | bytes 5242896 | tf_op jit(solution)/shard_map/all_gather | solution.py:40
  119.8 0.0 copy-done
  119.8 9.7 %convolution_convert_fusion = bf16[2048,1024]{1,0:T(8,128)(2,1)} fusion(bf16[2048,1280]{1,0:T(8,128)(2,1)} %all-gather.2.cloned.1.call-done, bf16[1280,1024]{1,0:T(8,128)(2,1)S(1)} %copy-done), kind=kOutput, calls=%fused_computation.13 | convolution fusion | flops 5370806272 | bytes 12058624 | tf_op jit(solution)/shard_map/dot_general | solution.py:39
  129.5 6.4 %copy.18 = bf16[8,256,1024]{1,2,0:T(8,128)(2,1)} copy(bf16[8,256,1024]{2,1,0:T(8,128)(2,1)} %bitcast.23) | data formatting | bytes 8388608 | tf_op jit(solution)/shard_map/all_to_all | solution.py:44
  136.0 96.4 %all_to_all.19 = bf16[8,256,1024]{1,2,0:T(8,128)(2,1)} all-to-all(bf16[8,256,1024]{1,2,0:T(8,128)(2,1)} %copy.18), channel_id=1, replica_groups=mesh['dp'=8,'tensor'=4] {'dp'}, dimensions={0} | all-to-all | bytes 8388608 | tf_op jit(solution)/shard_map/all_to_all | solution.py:44
  232.4 0.0 copy-start.2
  232.4 0.0 copy-start.5
  232.4 0.0 reduce-scatter.2.cloned.1.call-update
  232.5 0.6 copy-done.2
  233.0 0.3 fusion.23
  233.3 0.6 select_reduce_fusion
  236.6 0.7 select_reduce_fusion.2
  239.8 0.7 select_reduce_fusion.4
  243.1 0.7 select_reduce_fusion.6
  251.3 24.8 %reduce-scatter.2.cloned.1.call-done = bf16[256,2048]{0,1:T(8,128)(2,1)} async-done(((bf16[256,8192]{0,1:T(8,128)(2,1)}), bf16[256,2048]{0,1:T(8,128)(2,1)}) %reduce-scatter.2.cloned.1.call-update) | async-done | bytes 1048592 | tf_op jit(solution)/shard_map/reduce_scatter | solution.py:46
  276.1 0.0 copy-done.5
  276.1 2.5 add_convert_fusion
  278.6 2.3 copy.19
  280.9 0.0 copy-start.7
  280.9 2.0 dynamic-slice_bitcast_fusion
  282.9 1.4 collective-permute-start
  284.3 1.5 collective-permute-start.1
  285.8 2.4 collective-permute-start.2
  288.2 0.0 copy-done.7
  288.2 0.7 constant_dynamic-slice_fusion.1
  293.1 1.6 dynamic_update_slice.12
  294.7 0.5 collective-permute-done
  295.2 2.8 dynamic_update_slice.13
  298.0 0.0 collective-permute-done.1
  298.0 2.8 dynamic_update_slice.14
  300.8 9.9 %collective-permute-done.2 = bf16[64,2048]{1,0:T(8,128)(2,1)} collective-permute-done((bf16[64,2048]{1,0:T(8,128)(2,1)S(1)}, bf16[64,2048]{1,0:T(8,128)(2,1)}, u32[]{:S(2)}, u32[]{:S(2)}) %collective-permute-start.2) | collective-permute-done | bytes 262176 | tf_op jit(solution)/shard_map/ppermute | solution.py:12
  310.6 2.8 dynamic_update_slice.15
  313.4 0.0 copy-start.6
  313.4 4.4 %fusion.6 = (f32[512]{0:T(512)S(1)}, bf16[512,2048]{1,0:T(8,128)(2,1)}) fusion(bf16[512,2048]{1,0:T(8,128)(2,1)} %dynamic_update_slice.15, bf16[512,2048]{1,0:T(8,128)(2,1)} %param.18, pred[512]{0:T(512)(128)(4,1)S(1)} %iota_compare_fusion), kind=kLoop, calls=%fused_computation.10 | loop fusion | flops 4193792 | bytes 6294016 | tf_op jit(solution)/shard_map/reduce_sum | solution.py:78
  317.8 5.9 %psum.7 = f32[512]{0:T(512)S(1)} all-reduce(f32[512]{0:T(512)S(1)} %get-tuple-element.10), channel_id=1, replica_groups=mesh['dp'=8,'tensor'=4] {'tensor'}, use_global_device_ids=true, to_apply=%region_12.13 | all-reduce | flops 512 | bytes 4096 | tf_op jit(solution)/shard_map/psum | solution.py:78
  323.7 0.0 copy-done.6
  323.7 3.5 %fusion.8 = bf16[512,2048]{1,0:T(8,128)(2,1)} fusion(bf16[512,2048]{1,0:T(8,128)(2,1)} %get-tuple-element.11, f32[2048]{0:T(1024)S(1)} %copy-done.6, f32[512]{0:T(512)S(1)} %add_rsqrt_fusion.1), kind=kLoop, calls=%fused_computation.12 | loop fusion | flops 4194304 | bytes 4204544 | tf_op jit(solution)/shard_map/convert_element_type | solution.py:80
  (5 shorter events, 0.0 us)
Async XLA Ops:
  7.2 112.7 %copy-start = (bf16[1280,1024]{1,0:T(8,128)(2,1)S(1)}, bf16[1280,1024]{1,0:T(8,128)(2,1)}, u32[]{:S(2)}) copy-start(bf16[1280,1024]{1,0:T(8,128)(2,1)} %param.16) | copy-start | bytes 7864324
  7.2 112.7 %all-gather.2.cloned.1.call-start = ((), (), s32[]{:S(2)}) async-start(), calls=%async_computation.2 | async-start | bytes 5898240 | tf_op jit(solution)/shard_map/all_gather | solution.py:40
  7.2 2.7 copy-start.1
  9.9 0.8 copy-start.3
  9.9 0.8 copy-start.4
  13.3 5.3 %copy-start.8 = (f32[1280]{0:T(1024)S(1)}, f32[1280]{0:T(1024)}, u32[]{:S(2)}) copy-start(f32[1280]{0:T(1024)} %param.15) | copy-start | bytes 15364
  31.1 245.0 %reduce-scatter.2.cloned.1.call-start = ((), (), s32[]{:S(2)}) async-start(), calls=%async_computation.3 | async-start | bytes 5242880 | tf_op jit(solution)/shard_map/reduce_scatter | solution.py:46
  232.4 0.7 copy-start.2
  232.4 43.7 %copy-start.5 = (f32[2048]{0:T(1024)S(1)}, f32[2048]{0:T(1024)}, u32[]{:S(2)}) copy-start(f32[2048]{0:T(1024)} %param.17) | copy-start | bytes 24580
  280.9 7.3 %copy-start.7 = (s32[8,4,2]{0,2,1:T(2,128)S(1)}, s32[8,4,2]{0,2,1:T(2,128)}, u32[]{:S(2)}) copy-start(s32[8,4,2]{0,2,1:T(2,128)} %param.20) | copy-start | bytes 772
  282.9 12.3 %collective-permute-start = (bf16[64,2048]{1,0:T(8,128)(2,1)}, bf16[64,2048]{1,0:T(8,128)(2,1)}, u32[]{:S(2)}, u32[]{:S(2)}) collective-permute-start(bf16[64,2048]{1,0:T(8,128)(2,1)} %get-tuple-element.14), channel_id=1, source_target_pairs={{28,0},{0,4},{4,8},{8,12},{12,16},{16,20},{20,24},{24,28},{29,1},{... | collective-permute-start | bytes 786440 | tf_op jit(solution)/shard_map/ppermute | solution.py:12
  284.3 13.7 %collective-permute-start.1 = (bf16[64,2048]{1,0:T(8,128)(2,1)S(1)}, bf16[64,2048]{1,0:T(8,128)(2,1)}, u32[]{:S(2)}, u32[]{:S(2)}) collective-permute-start(bf16[64,2048]{1,0:T(8,128)(2,1)S(1)} %get-tuple-element.13), channel_id=1, source_target_pairs={{24,0},{28,4},{0,8},{4,12},{8,16},{12,20},{16,24},{20,28},{25,1},{... | collective-permute-start | bytes 786440 | tf_op jit(solution)/shard_map/ppermute | solution.py:12
  285.8 24.8 %collective-permute-start.2 = (bf16[64,2048]{1,0:T(8,128)(2,1)S(1)}, bf16[64,2048]{1,0:T(8,128)(2,1)}, u32[]{:S(2)}, u32[]{:S(2)}) collective-permute-start(bf16[64,2048]{1,0:T(8,128)(2,1)S(1)} %get-tuple-element.12), channel_id=1, source_target_pairs={{20,0},{24,4},{28,8},{0,12},{4,16},{8,20},{12,24},{16,28},{21,1},{... | collective-permute-start | bytes 786440 | tf_op jit(solution)/shard_map/ppermute | solution.py:12
  313.4 10.2 %copy-start.6 = (f32[2048]{0:T(1024)S(1)}, f32[2048]{0:T(1024)}, u32[]{:S(2)}) copy-start(f32[2048]{0:T(1024)} %param.19) | copy-start | bytes 24580
Sparse Core Ops, SparseCore 0:
  31.2 88.5 all-gather.1
  232.5 43.5 reduce-scatter.1
where the time goes:
time: 335 us; the launch traced here: 334 us
  waiting for transfers between devices  124 us (37%)
  blocking collectives  102 us (30%)
  between operations  33.7 us (10%)
  local copies, waits for them, and re-layouts  27.5 us (8%)
  matrix products  22.2 us (7%)
  other arithmetic  19.1 us (6%)
  starting transfers between devices  5.41 us (2%)
    all_to_all x1, blocking collectives, per_device(): lax.all_to_all(partial_value, 'dp', split_axis=0, concat_axis=1, tiled=True)  96.4 us
    all_gather x1, waiting for transfers between devices, per_device(): lax.all_gather(hidden, 'dp', axis=0, tiled=True)  88.7 us
    reduce_scatter x1, waiting for transfers between devices, per_device(): lax.psum_scatter(partial_terms.astype(jnp.bfloat16), 'tensor', scatter_di...  24.8 us
    dot_general x1, matrix products, per_device(): jnp.dot(merged, first_weight, preferred_element_type=jnp.float32)  12.5 us
    ppermute x3, waiting for transfers between devices, passed_along(): return lax.ppermute(block, axis, route)  10.3 us
    dynamic_update_slice x4, local copies, waits for them, and re-layouts, per_device(): lax.dynamic_update_slice(image_rows, incoming, (filled_rows, zero_index))  9.95 us
    dot_general x1, matrix products, per_device(): jnp.dot(lax.all_gather(hidden, 'dp', axis=0, tiled=True), second_weight,...  9.71 us
  transfers between devices with their start and end apart: 5, of which 4 were waited for; matrix products, arithmetic and copies ran while one was open for 3% of the time, Pallas kernels for 0%

commit v1 on v0

--- a/solution.py
+++ b/solution.py
@@ -41,7 +41,12 @@
         second_weight,
         preferred_element_type=jnp.float32,
     ).astype(jnp.bfloat16)
-    columns = lax.all_to_all(partial_value, "dp", split_axis=0, concat_axis=1, tiled=True)
+    columns = jnp.concatenate(
+        lax.all_to_all(
+            jnp.stack(jnp.split(partial_value, lax.axis_size("dp"), axis=0)), "dp", 0, 0
+        ),
+        axis=1,
+    )
     partial_terms = columns.astype(jnp.float32)
     summed = lax.psum_scatter(
         partial_terms.astype(jnp.bfloat16), "tensor", scatter_dimension=1, tiled=True

time: 335 us -> 333 us (level)
    all_to_all x1 -> x0, local copies, waits for them, and re-layouts: 6.45 us -> none  [per_device(): lax.all_to_all(partial_value, 'dp', split_axis=0, concat_axis=1, tiled=True)]
    reshape x0 -> x1, local copies, waits for them, and re-layouts: none -> 6.43 us  [per_device(): jnp.concatenate(lax.all_to_all(jnp.stack(jnp.split(partial_value, lax.axi...]
where the time goes in v1:
time: 333 us; the launch traced here: 332 us
  waiting for transfers between devices  124 us (37%)
  blocking collectives  102 us (31%)
  between operations  33.7 us (10%)
  local copies, waits for them, and re-layouts  27.8 us (8%)
  matrix products  20.8 us (6%)
  other arithmetic  19.1 us (6%)
  starting transfers between devices  5.46 us (2%)
    all_to_all x1, blocking collectives, per_device(): lax.all_to_all(jnp.stack(jnp.split(partial_value, lax.axis_size('dp'), ax...  96.1 us
    all_gather x1, waiting for transfers between devices, per_device(): lax.all_gather(hidden, 'dp', axis=0, tiled=True)  88.7 us
    reduce_scatter x1, waiting for transfers between devices, per_device(): lax.psum_scatter(partial_terms.astype(jnp.bfloat16), 'tensor', scatter_di...  24.6 us
    dot_general x1, matrix products, per_device(): jnp.dot(merged, first_weight, preferred_element_type=jnp.float32)  12.5 us
    ppermute x3, waiting for transfers between devices, passed_along(): return lax.ppermute(block, axis, route)  10.3 us
    dynamic_update_slice x4, local copies, waits for them, and re-layouts, per_device(): lax.dynamic_update_slice(image_rows, incoming, (filled_rows, zero_index))  9.95 us
    dot_general x1, matrix products, per_device(): jnp.dot(lax.all_gather(hidden, 'dp', axis=0, tiled=True), second_weight,...  8.3 us
  transfers between devices with their start and end apart: 5, of which 4 were waited for; matrix products, arithmetic and copies ran while one was open for 3% of the time, Pallas kernels for 0%

profile of v1, /device:TPU:0, one launch (start us, length us, event | category | flops | bytes accessed | tf_op | source)
XLA Modules:
  0.0 332.5 jit_solution(9564299911129974610)
XLA Ops:
  7.2 0.0 copy-start
  7.2 0.0 copy-start.3
  7.2 0.0 all-gather.2.cloned.1.call-start
  7.2 0.0 copy-start.1
  7.2 0.0 copy-start.4
  7.3 2.3 convert_reduce_fusion
  9.6 0.3 copy-done.1
  9.9 0.8 fusion.2
  10.7 0.0 copy-done.3
  10.8 0.0 copy-done.4
  10.8 2.5 fusion.5
  13.3 0.0 copy-start.8
  13.3 5.2 %convert_element_type.31 = bf16[256,5120]{1,0:T(8,128)(2,1)} reshape(bf16[1024,1280]{1,0:T(8,128)(2,1)} %fusion.5) | data formatting | bytes 5242880 | tf_op jit(solution)/shard_map/convert_element_type | solution.py:32
  18.5 0.0 copy-done.8
  18.5 12.5 %fusion.11 = bf16[256,1280]{1,0:T(8,128)(2,1)} fusion(bf16[256,5120]{1,0:T(8,128)(2,1)} %convert_element_type.31, bf16[5120,1280]{1,0:T(8,128)(2,1)} %param.14, f32[1280]{0:T(1024)S(1)} %copy-done.8), kind=kOutput, calls=%fused_computation.20 | convolution fusion | flops 3377070080 | bytes 16389120 | tf_op jit(solution)/shard_map/dot_general | solution.py:34
  31.1 0.0 all-gather.2.cloned.1.call-update
  31.1 0.0 reduce-scatter.2.cloned.1.call-start
  31.1 88.7 %all-gather.2.cloned.1.call-done = bf16[2048,1280]{1,0:T(8,128)(2,1)} async-done(((bf16[256,1280]{1,0:T(8,128)(2,1)}), bf16[2048,1280]{1,0:T(8,128)(2,1)}) %all-gather.2.cloned.1.call-update) | async-done | bytes 5242896 | tf_op jit(solution)/shard_map/all_gather | solution.py:40
  119.8 0.0 copy-done
  119.8 8.3 %convolution_convert_fusion = bf16[2048,1024]{1,0:T(8,128)(2,1)S(1)} fusion(bf16[2048,1280]{1,0:T(8,128)(2,1)} %all-gather.2.cloned.1.call-done, bf16[1280,1024]{1,0:T(8,128)(2,1)S(1)} %copy-done), kind=kOutput, calls=%fused_computation.13 | convolution fusion | flops 5370806272 | bytes 12058624 | tf_op jit(solution)/shard_map/dot_general | solution.py:39
  128.5 96.1 %all_to_all.5 = bf16[8,256,1024]{2,1,0:T(8,128)(2,1)} all-to-all(bf16[8,256,1024]{2,1,0:T(8,128)(2,1)S(1)} %fusion.19), channel_id=1, replica_groups=mesh['dp'=8,'tensor'=4] {'dp'}, dimensions={0} | all-to-all | bytes 8388608 | tf_op jit(solution)/shard_map/all_to_all | solution.py:45
  224.6 6.4 %copy.18 = bf16[256,8,1024]{0,2,1:T(8,128)(2,1)} copy(bf16[256,8,1024]{2,0,1:T(8,128)(2,1)} %bitcast.52) | data formatting | bytes 8388608 | tf_op jit(solution)/shard_map/reshape | solution.py:44
  231.1 0.0 copy-start.2
  231.1 0.0 copy-start.5
  231.1 0.0 reduce-scatter.2.cloned.1.call-update
  231.2 0.6 copy-done.2
  231.7 0.3 fusion.31
  232.0 0.6 select_reduce_fusion
  235.3 0.7 select_reduce_fusion.2
  238.5 0.7 select_reduce_fusion.4
  241.8 0.7 select_reduce_fusion.6
  250.0 24.6 %reduce-scatter.2.cloned.1.call-done = bf16[256,2048]{0,1:T(8,128)(2,1)} async-done(((bf16[256,8192]{0,1:T(8,128)(2,1)}), bf16[256,2048]{0,1:T(8,128)(2,1)}) %reduce-scatter.2.cloned.1.call-update) | async-done | bytes 1048592 | tf_op jit(solution)/shard_map/reduce_scatter | solution.py:51
  274.6 0.0 copy-done.5
  274.6 2.5 add_convert_fusion
  277.1 0.0 copy-start.7
  277.1 2.3 copy.19
  279.4 2.0 dynamic-slice_bitcast_fusion
  281.3 1.5 collective-permute-start
  282.8 1.5 collective-permute-start.1
  284.3 2.4 collective-permute-start.2
  286.7 0.0 copy-done.7
  286.7 0.7 constant_dynamic-slice_fusion.1
  291.7 1.6 dynamic_update_slice.12
  293.2 0.4 collective-permute-done
  293.6 2.8 dynamic_update_slice.13
  296.4 0.0 collective-permute-done.1
  296.4 2.8 dynamic_update_slice.14
  299.2 9.9 %collective-permute-done.2 = bf16[64,2048]{1,0:T(8,128)(2,1)} collective-permute-done((bf16[64,2048]{1,0:T(8,128)(2,1)S(1)}, bf16[64,2048]{1,0:T(8,128)(2,1)}, u32[]{:S(2)}, u32[]{:S(2)}) %collective-permute-start.2) | collective-permute-done | bytes 262176 | tf_op jit(solution)/shard_map/ppermute | solution.py:12
  309.1 2.8 dynamic_update_slice.15
  311.9 0.0 copy-start.6
  311.9 4.4 %fusion.6 = (f32[512]{0:T(512)S(1)}, bf16[512,2048]{1,0:T(8,128)(2,1)}) fusion(bf16[512,2048]{1,0:T(8,128)(2,1)} %dynamic_update_slice.15, bf16[512,2048]{1,0:T(8,128)(2,1)} %param.18, pred[512]{0:T(512)(128)(4,1)S(1)} %iota_compare_fusion), kind=kLoop, calls=%fused_computation.10 | loop fusion | flops 4193792 | bytes 6294016 | tf_op jit(solution)/shard_map/reduce_sum | solution.py:83
  316.3 5.9 %psum.7 = f32[512]{0:T(512)S(1)} all-reduce(f32[512]{0:T(512)S(1)} %get-tuple-element.10), channel_id=1, replica_groups=mesh['dp'=8,'tensor'=4] {'tensor'}, use_global_device_ids=true, to_apply=%region_12.13 | all-reduce | flops 512 | bytes 4096 | tf_op jit(solution)/shard_map/psum | solution.py:83
  322.2 0.0 copy-done.6
  322.2 3.5 %fusion.8 = bf16[512,2048]{1,0:T(8,128)(2,1)} fusion(bf16[512,2048]{1,0:T(8,128)(2,1)} %get-tuple-element.11, f32[2048]{0:T(1024)S(1)} %copy-done.6, f32[512]{0:T(512)S(1)} %add_rsqrt_fusion.1), kind=kLoop, calls=%fused_computation.12 | loop fusion | flops 4194304 | bytes 4204544 | tf_op jit(solution)/shard_map/convert_element_type | solution.py:85
  (13 shorter events, 0.3 us)
Async XLA Ops:
  7.2 112.7 %copy-start = (bf16[1280,1024]{1,0:T(8,128)(2,1)S(1)}, bf16[1280,1024]{1,0:T(8,128)(2,1)}, u32[]{:S(2)}) copy-start(bf16[1280,1024]{1,0:T(8,128)(2,1)} %param.16) | copy-start | bytes 7864324
  7.2 3.6 %copy-start.3 = (f32[1280]{0:T(1024)S(1)}, f32[1280]{0:T(1024)}, u32[]{:S(2)}) copy-start(f32[1280]{0:T(1024)} %param.13) | copy-start | bytes 15364
  7.2 112.6 %all-gather.2.cloned.1.call-start = ((), (), s32[]{:S(2)}) async-start(), calls=%async_computation.2 | async-start | bytes 5898240 | tf_op jit(solution)/shard_map/all_gather | solution.py:40
  7.2 2.7 copy-start.1
  7.2 3.5 %copy-start.4 = (f32[1280]{0:T(1024)S(1)}, f32[1280]{0:T(1024)}, u32[]{:S(2)}) copy-start(f32[1280]{0:T(1024)} %param.12) | copy-start | bytes 15364
  13.3 5.3 %copy-start.8 = (f32[1280]{0:T(1024)S(1)}, f32[1280]{0:T(1024)}, u32[]{:S(2)}) copy-start(f32[1280]{0:T(1024)} %param.15) | copy-start | bytes 15364
  31.1 243.5 %reduce-scatter.2.cloned.1.call-start = ((), (), s32[]{:S(2)}) async-start(), calls=%async_computation.3 | async-start | bytes 5242880 | tf_op jit(solution)/shard_map/reduce_scatter | solution.py:51
  231.1 0.7 copy-start.2
  231.1 43.5 %copy-start.5 = (f32[2048]{0:T(1024)S(1)}, f32[2048]{0:T(1024)}, u32[]{:S(2)}) copy-start(f32[2048]{0:T(1024)} %param.17) | copy-start | bytes 24580
  277.1 9.6 %copy-start.7 = (s32[8,4,2]{0,2,1:T(2,128)S(1)}, s32[8,4,2]{0,2,1:T(2,128)}, u32[]{:S(2)}) copy-start(s32[8,4,2]{0,2,1:T(2,128)} %param.20) | copy-start | bytes 772
  281.3 12.3 %collective-permute-start = (bf16[64,2048]{1,0:T(8,128)(2,1)}, bf16[64,2048]{1,0:T(8,128)(2,1)}, u32[]{:S(2)}, u32[]{:S(2)}) collective-permute-start(bf16[64,2048]{1,0:T(8,128)(2,1)} %get-tuple-element.14), channel_id=1, source_target_pairs={{28,0},{0,4},{4,8},{8,12},{12,16},{16,20},{20,24},{24,28},{29,1},{... | collective-permute-start | bytes 786440 | tf_op jit(solution)/shard_map/ppermute | solution.py:12
  282.8 13.6 %collective-permute-start.1 = (bf16[64,2048]{1,0:T(8,128)(2,1)S(1)}, bf16[64,2048]{1,0:T(8,128)(2,1)}, u32[]{:S(2)}, u32[]{:S(2)}) collective-permute-start(bf16[64,2048]{1,0:T(8,128)(2,1)S(1)} %get-tuple-element.13), channel_id=1, source_target_pairs={{24,0},{28,4},{0,8},{4,12},{8,16},{12,20},{16,24},{20,28},{25,1},{... | collective-permute-start | bytes 786440 | tf_op jit(solution)/shard_map/ppermute | solution.py:12
  284.3 24.8 %collective-permute-start.2 = (bf16[64,2048]{1,0:T(8,128)(2,1)S(1)}, bf16[64,2048]{1,0:T(8,128)(2,1)}, u32[]{:S(2)}, u32[]{:S(2)}) collective-permute-start(bf16[64,2048]{1,0:T(8,128)(2,1)S(1)} %get-tuple-element.12), channel_id=1, source_target_pairs={{20,0},{24,4},{28,8},{0,12},{4,16},{8,20},{12,24},{16,28},{21,1},{... | collective-permute-start | bytes 786440 | tf_op jit(solution)/shard_map/ppermute | solution.py:12
  311.9 10.3 %copy-start.6 = (f32[2048]{0:T(1024)S(1)}, f32[2048]{0:T(1024)}, u32[]{:S(2)}) copy-start(f32[2048]{0:T(1024)} %param.19) | copy-start | bytes 24580
Sparse Core Ops, SparseCore 0:
  31.2 88.5 all-gather.1
  231.2 43.2 reduce-scatter.1
